TPU v7x, 32 devices: a whole 2x2x4 slice. The times are simulated.
32 devices in a mesh: grp: 2 (over x), space: 16 (over z, y, core).
Axes of the slice: x: 2, y: 2, z: 4, core: 2. Of those that a mesh axis runs over, the one named last changes fastest.
Arguments:
- propagator: bfloat16 [4, 3, 4, 12, 32768], P('grp', None, None, None, 'space'), parts along dimension 0, may hold values from -6 to 6
- eigvecs: bfloat16 [4, 3, 256, 32768], P('grp', None, None, 'space'), parts along dimension 0, may hold values from -6 to 6
- operator_weights: float32 [256, 2, 256], P('grp'), parts along dimension 0, may hold values from -0.375 to 0.375
- sink_time: int32 [2], P('grp'), parts along dimension 0, may hold values from 0 to 127
- term_index: int32 [48, 3], replicated, may hold values from 0 to 11
- term_sign: int32 [48], replicated, may hold values from 0 to 1
- solver_order: int32 [32768], P('space'), may hold values from 0 to 32767, as said below
Outputs:
- solver_source: bfloat16 [4, 3, 4, 12, 32768], P('grp', None, None, None, 'space'), parts along dimension 0
There are 2 independent parts, one for each index of `grp`. A program takes and returns all parts, laid end to end along the dimension named above; an argument that names none is the same for every part. Nothing has to cross between parts.
Inputs may be any that keep to these rules, and one draw needn't show every extreme that they name: solver_order is a permutation of the sites; split into blocks of 2048 positions and each block into pieces of 128, piece d of block e holds only sites d * 2048 to (d + 1) * 2048 - 1.
All inputs are finite; a program needn't handle non-finite values.
Results may differ from a plain program's by a relative error of at most 0.006.
Values may be sent and summed in bfloat16 or wider, within the bound.
A program may use at most 64 MiB of HBM per device.

v0:
```python
import math
import jax
import jax.numpy as jnp
from jax import lax
from jax.sharding import PartitionSpec as P

NVEC = 256
NMOM = 4
EXTENT = 64
MOMENTA = ((0, 0, 0), (1, 0, 0), (0, 1, 0), (0, 0, 1))
PRECISE = lax.Precision.HIGHEST


def phase_tables(offset, length):
    site_index = offset + jnp.arange(length, dtype=jnp.int32)
    coord_x = site_index % EXTENT
    coord_y = site_index // EXTENT % EXTENT
    coord_z = site_index // (EXTENT * EXTENT)
    windings = jnp.stack(
        [
            (step_x * coord_x + step_y * coord_y + step_z * coord_z) % EXTENT
            for step_x, step_y, step_z in MOMENTA
        ]
    )
    angles = windings.astype(jnp.float32) * (2.0 * math.pi / EXTENT)
    return (jnp.cos(angles), jnp.sin(angles))


def phased_rows(prop_colour, cosine_table, sine_table):
    real_part = prop_colour[0].astype(jnp.float32)[None]
    imag_part = prop_colour[1].astype(jnp.float32)[None]
    cos_rows = cosine_table[:, None, None, :]
    sin_rows = sine_table[:, None, None, :]
    turned = jnp.stack(
        [cos_rows * real_part + sin_rows * imag_part, cos_rows * imag_part - sin_rows * real_part]
    )
    return turned.astype(jnp.bfloat16).reshape(-1, turned.shape[-1])


def project(eig_colour, phased, scale_in):
    site_dims = (((1,), (1,)), ((), ()))
    from_real = lax.dot_general(
        eig_colour[0], phased, site_dims, preferred_element_type=jnp.float32
    ).reshape(-1, 2, NMOM, 48)
    from_imag = lax.dot_general(
        eig_colour[1], phased, site_dims, preferred_element_type=jnp.float32
    ).reshape(-1, 2, NMOM, 48)
    real_part = from_real[:, 0] + from_imag[:, 1]
    imag_part = from_real[:, 1] - from_imag[:, 0]
    return jnp.stack([real_part, imag_part]) * scale_in


def assemble(pieces):
    stacked = jnp.stack(pieces)
    vectors = stacked.shape[2]
    return stacked.transpose(3, 1, 2, 0, 4).reshape(NMOM, 2, vectors, 144)


def weighted_total(blocks, weights):
    real_sum = jnp.einsum("k,pkc->pc", weights[0], blocks[:, 0], precision=PRECISE) - jnp.einsum(
        "k,pkc->pc", weights[1], blocks[:, 1], precision=PRECISE
    )
    imag_sum = jnp.einsum("k,pkc->pc", weights[0], blocks[:, 1], precision=PRECISE) + jnp.einsum(
        "k,pkc->pc", weights[1], blocks[:, 0], precision=PRECISE
    )
    return jnp.stack([real_sum, imag_sum], axis=1)


def term_tables(term_index, term_sign):
    channels = jnp.arange(12, dtype=jnp.int32)
    first_pick = (term_index[:, 0:1] == channels[None]).astype(jnp.float32)
    second_pick = (term_index[:, 1:2] == channels[None]).astype(jnp.float32)
    sign_values = (2 * term_sign - 1).astype(jnp.float32)
    placement = (term_index[None, :, 2] == channels[:, None]).astype(jnp.float32) * sign_values[
        None
    ]
    return (first_pick, second_pick, placement)


def contract(blocks, weighted, first_pick, second_pick, placement):
    vectors = blocks.shape[2]
    block_grid = blocks.reshape(NMOM, 2, vectors, 12, 12)
    first_terms = jnp.einsum("mi,pqkij->pqkmj", first_pick, block_grid, precision=PRECISE)
    second_terms = jnp.einsum(
        "mi,pqij->pqmj", second_pick, weighted.reshape(NMOM, 2, 12, 12), precision=PRECISE
    )[:, :, None]
    real_part = first_terms[:, 0] * second_terms[:, 0] - first_terms[:, 1] * second_terms[:, 1]
    imag_part = first_terms[:, 0] * second_terms[:, 1] + first_terms[:, 1] * second_terms[:, 0]
    product = jnp.stack([real_part, imag_part], axis=1)
    return jnp.einsum("cm,pqkmj->pqkcj", placement, product, precision=PRECISE).reshape(
        NMOM, 2, vectors, 144
    )


def rebuild(coeffs, eig_colour, colour, cosine_table, sine_table, scale_out):
    vectors = coeffs.shape[2]
    colour_block = coeffs.reshape(NMOM, 2, vectors, 3, 48)[:, :, :, colour]
    coeff_table = colour_block.transpose(2, 1, 0, 3).reshape(vectors, 2 * NMOM * 48)
    vector_dims = (((0,), (0,)), ((), ()))
    from_real = lax.dot_general(
        coeff_table, eig_colour[0], vector_dims, preferred_element_type=jnp.float32
    ).reshape(2, NMOM, 48, -1)
    from_imag = lax.dot_general(
        coeff_table, eig_colour[1], vector_dims, preferred_element_type=jnp.float32
    ).reshape(2, NMOM, 48, -1)
    real_part = from_real[0] - from_imag[1]
    imag_part = from_real[1] + from_imag[0]
    cos_rows = cosine_table[:, None, :]
    sin_rows = sine_table[:, None, :]
    out_real = jnp.sum(cos_rows * real_part - sin_rows * imag_part, axis=0)
    out_imag = jnp.sum(cos_rows * imag_part + sin_rows * real_part, axis=0)
    return jnp.stack([out_real, out_imag]) * scale_out


def on_device(
    propagator, eigvecs, operator_weights, sink_time, term_index, term_sign, solver_order
):
    length = propagator.shape[-1]
    devices = lax.axis_size("space")
    offset = lax.axis_index("space") * length
    cosine_table, sine_table = phase_tables(offset, length)
    scale_in = 1.0 / math.sqrt(3.0 * length * devices)
    pieces = []
    for colour in range(3):
        phased = phased_rows(propagator[:, colour], cosine_table, sine_table)
        pieces.append(project(eigvecs[:, colour], phased, scale_in))
    partial_blocks = assemble(pieces)
    weights = lax.dynamic_index_in_dim(operator_weights, sink_time[0], 0, keepdims=False)
    first_pick, second_pick, placement = term_tables(term_index, term_sign)
    blocks = lax.psum(partial_blocks, "space")
    weighted = weighted_total(blocks, weights)
    coeffs = contract(blocks, weighted, first_pick, second_pick, placement).astype(jnp.bfloat16)
    scale_out = 1.0 / math.sqrt(NMOM * NVEC)
    colours = [
        rebuild(coeffs, eigvecs[:, colour], colour, cosine_table, sine_table, scale_out)
        for colour in range(3)
    ]
    source = jnp.stack(colours, axis=1).astype(jnp.bfloat16).reshape(2 * 3 * 48, length)
    wanted = lax.all_to_all(
        solver_order.reshape(devices, -1), "space", split_axis=0, concat_axis=0, tiled=True
    )
    local_index = wanted.reshape(length) - offset
    picked = jnp.take(source, local_index, axis=1)
    placed = lax.all_to_all(picked, "space", split_axis=1, concat_axis=1, tiled=True)
    return placed.reshape(2, 3, 4, 12, length)


def solution(mesh):
    return jax.shard_map(
        on_device,
        mesh=mesh,
        in_specs=(
            P("grp", None, None, None, "space"),
            P("grp", None, None, "space"),
            P("grp", None, None),
            P("grp"),
            P(),
            P(),
            P("space"),
        ),
        out_specs=P("grp", None, None, None, "space"),
        check_vma=False,
    )
```

profile of v0, /device:TPU:0, one launch (start us, length us, event | category | flops | bytes accessed | tf_op | source)
XLA Modules:
  0.0 206.0 jit_solution(521534441980782932)
XLA Ops:
  6.8 1.5 bitcast_convert_fusion.5
  8.6 0.2 copy.38
  9.8 0.3 fusion.77
  10.0 2.7 %add_convert_fusion.2 = (bf16[1,4,4,12,2048]{4,3,2,1,0:T(8,128)(2,1)S(1)}, bf16[1,4,4,12,2048]{4,3,2,1,0:T(8,128)(2,1)S(1)}, bf16[1,4,4,12,2048]{4,3,2,1,0:T(8,1...) fusion(f32[4,12,2048]{2,1,0:T(8,128)S(1)} %copy.38, ...), kind=kLoop, calls=%fused_computation.16 | loop fusion | flops 9437184 | bytes 7143424 | tf_op jit(solution)/shard_map/convert.13
  12.8 0.3 pad_maximum_fusion
  13.1 1.4 convert_element_type.148
  14.4 3.2 %fusion.33 = f32[384,256]{1,0:T(8,128)} fusion(bf16[384,2048]{1,0:T(8,128)(2,1)} %convert_element_type.148, bf16[2,3,256,2048]{3,2,1,0:T(8,128)(2,1)} %param.8), kind=kOutput, calls=%fused_computation.58 | convolution fusion | flops 402653184 | bytes 3014656 | tf_op jit(solution)/shard_map/dot_general | solution.py:42
  17.6 2.7 %fusion.29 = f32[384,256]{1,0:T(8,128)} fusion(bf16[384,2048]{1,0:T(8,128)(2,1)S(1)} %copy-done.6, bf16[2,3,256,2048]{3,2,1,0:T(8,128)(2,1)} %param.8), kind=kOutput, calls=%fused_computation.54 | convolution fusion | flops 402653184 | bytes 3014656 | tf_op jit(solution)/shard_map/dot_general | solution.py:45
  20.4 0.3 pad_maximum_fusion.1
  20.6 1.4 convert_element_type.153
  22.0 3.2 %fusion.25 = f32[384,256]{1,0:T(8,128)} fusion(bf16[384,2048]{1,0:T(8,128)(2,1)} %convert_element_type.153, bf16[2,3,256,2048]{3,2,1,0:T(8,128)(2,1)} %param.8), kind=kOutput, calls=%fused_computation.50 | convolution fusion | flops 402653184 | bytes 3014656 | tf_op jit(solution)/shard_map/dot_general | solution.py:42
  25.2 2.7 %fusion.21 = f32[384,256]{1,0:T(8,128)} fusion(bf16[384,2048]{1,0:T(8,128)(2,1)S(1)} %copy-done.7, bf16[2,3,256,2048]{3,2,1,0:T(8,128)(2,1)} %param.8), kind=kOutput, calls=%fused_computation.46 | convolution fusion | flops 402653184 | bytes 3014656 | tf_op jit(solution)/shard_map/dot_general | solution.py:45
  27.9 0.3 pad_maximum_fusion.2
  28.2 1.4 convert_element_type.158
  29.5 2.4 %fusion.17 = f32[384,256]{1,0:T(8,128)S(1)} fusion(bf16[384,2048]{1,0:T(8,128)(2,1)} %convert_element_type.158, bf16[2,3,256,2048]{3,2,1,0:T(8,128)(2,1)} %param.8), kind=kOutput, calls=%fused_computation.42 | convolution fusion | flops 402653184 | bytes 3014656 | tf_op jit(solution)/shard_map/dot_general | solution.py:42
  32.0 1.9 fusion.13
  34.0 0.8 copy-done.9
  35.2 1.1 pad_maximum_fusion.3
  36.4 7.4 %all-to-all-start = ((s32[16,1,128]{2,1,0:T(1,128)}), s32[16,1,128]{2,1,0:T(1,128)S(1)}, u32[]{:S(2)}, u32[]{:S(2)}) async-start(s32[16,1,128]{2,1,0:T(1,128)} %bitcast), calls=%async_computation | async-start | bytes 16384 | tf_op jit(solution)/shard_map/all_to_all | solution.py:139
  44.5 5.7 %all-to-all-done = s32[16,1,128]{2,1,0:T(1,128)S(1)} async-done(((s32[16,1,128]{2,1,0:T(1,128)}), s32[16,1,128]{2,1,0:T(1,128)S(1)}, u32[]{:S(2)}, u32[]{:S(2)}) %all-to-all-start) | async-done | bytes 8224 | tf_op jit(solution)/shard_map/all_to_all | solution.py:139
  50.2 83.1 %all-reduce.2.cloned.1.call-done = f32[4,2,256,144]{2,3,1,0:T(8,128)} async-done(((f32[4,2,256,144]{2,3,1,0:T(8,128)}), f32[4,2,256,144]{2,3,1,0:T(8,128)}) %all-reduce.2.cloned.1.call-update) | async-done | bytes 1179664 | tf_op jit(solution)/shard_map/psum | solution.py:130
  133.4 1.7 fusion.51
  135.1 1.7 fusion.53
  137.0 0.6 fusion.50
  137.6 0.6 fusion.52
  138.6 0.9 copy.46
  139.5 2.1 %convolution_bitcast_fusion = f32[4,2,256,48,12]{2,3,4,1,0:T(8,128)S(1)} fusion(f32[4,2,256,12,12]{2,1,4,3,0:T(2,128)S(1)} %bitcast.204, s32[48]{0:T(128)S(1)} %get-tuple-element.55), kind=kOutput, calls=%fused_computation.7 | convolution fusion | flops 169869888 | bytes 5898432 | tf_op jit(solution)/shard_map/mi,pqkij->pqkmj/dot_general | solution.py:83
  141.7 0.9 multiply_subtract_fusion
  142.5 2.5 %fusion.8 = bf16[4,2,256,12,12]{2,3,4,1,0:T(8,128)(2,1)S(1)} fusion(f32[4,1,256,48,12]{2,3,4,1,0:T(8,128)S(1)} %get-tuple-element.24, f32[4,1,256,48,12]{2,3,4,1,0:T(8,128)S(1)} %get-tuple-element.23, f32[48]{0:T(128)S(1)} %add_convert_fusion.4, s32[48]{0:T(128)S(1)} %get-tuple-element.54), kind=kOutput, calls=%fused_computation.31 | convolution fusion | flops 171345024 | bytes 5308800 | tf_op jit(solution)/shard_map/cm,pqkmj->pqkcj/dot_general | solution.py:90
  145.1 0.6 copy.50
  145.7 0.5 fusion.86
  146.3 0.6 fusion.11
  146.8 0.6 fusion.15
  147.5 0.6 fusion.19
  148.0 0.6 fusion.23
  148.7 0.6 fusion.27
  149.2 0.6 fusion.31
  149.8 0.6 slice_add_fusion
  150.5 0.7 slice_add_fusion.1
  151.2 0.7 slice_subtract_fusion.2
  151.8 1.4 subtract_reduce_fusion.2
  153.6 0.8 copy.57
  154.4 7.5 %gather_fusion = bf16[2048,288]{1,0:T(8,128)(2,1)S(1)} fusion(bf16[288,2048]{0,1:T(8,128)(2,1)S(1)} %copy.57, s32[2048]{0:T(1024)S(1)} %broadcast_clamp_fusion), kind=kCustom, calls=%fused_computation | custom fusion | bytes 2367488 | tf_op jit(solution)/shard_map/jit(_take)/gather | solution.py:143
  161.9 0.9 copy.58
  162.9 33.0 %all_to_all.15 = bf16[288,16,128]{2,0,1:T(8,128)(2,1)S(1)} all-to-all(bf16[288,16,128]{2,0,1:T(8,128)(2,1)S(1)} %broadcast_select_fusion), channel_id=1, replica_groups=mesh['grp'=2,'space'=16] {'space'}, dimensions={1} | all-to-all | bytes 2359296 | tf_op jit(solution)/shard_map/all_to_all | solution.py:144
  195.9 0.5 copy.59
  196.4 0.8 reshape.956
  197.2 1.9 copy.60
  (71 shorter events, 2.9 us)
Async XLA Ops:
  6.5 126.8 %copy-start = (f32[128,2,256]{2,1,0:T(2,128)S(1)}, f32[128,2,256]{2,1,0:T(2,128)}, u32[]{:S(2)}) copy-start(f32[128,2,256]{2,1,0:T(2,128)} %param.9) | copy-start | bytes 786436
  6.5 126.8 %all-reduce.2.cloned.1.call-start = ((), (), s32[]{:S(2)}) async-start(), calls=%async_computation.2 | async-start | bytes 2359296 | tf_op jit(solution)/shard_map/psum | solution.py:130
  14.4 3.2 %copy-start.6 = (bf16[384,2048]{1,0:T(8,128)(2,1)S(1)}, bf16[384,2048]{1,0:T(8,128)(2,1)}, u32[]{:S(2)}) copy-start(bf16[384,2048]{1,0:T(8,128)(2,1)} %convert_element_type.148) | copy-start | bytes 4718596
  17.6 2.7 %copy-start.4 = (bf16[1,4,4,12,2048]{4,3,2,1,0:T(8,128)(2,1)S(1)}, bf16[1,4,4,12,2048]{4,3,2,1,0:T(8,128)(2,1)}, u32[]{:S(2)}) copy-start(bf16[1,4,4,12,2048]{4,3,2,1,0:T(8,128)(2,1)} %get-tuple-element.48) | copy-start | bytes 2359300
  17.6 2.7 %copy-start.5 = (bf16[1,4,4,12,2048]{4,3,2,1,0:T(8,128)(2,1)S(1)}, bf16[1,4,4,12,2048]{4,3,2,1,0:T(8,128)(2,1)}, u32[]{:S(2)}) copy-start(bf16[1,4,4,12,2048]{4,3,2,1,0:T(8,128)(2,1)} %get-tuple-element.49) | copy-start | bytes 2359300
  22.0 3.2 %copy-start.7 = (bf16[384,2048]{1,0:T(8,128)(2,1)S(1)}, bf16[384,2048]{1,0:T(8,128)(2,1)}, u32[]{:S(2)}) copy-start(bf16[384,2048]{1,0:T(8,128)(2,1)} %convert_element_type.153) | copy-start | bytes 4718596
  25.2 2.7 %copy-start.3 = (bf16[1,4,4,12,2048]{4,3,2,1,0:T(8,128)(2,1)S(1)}, bf16[1,4,4,12,2048]{4,3,2,1,0:T(8,128)(2,1)}, u32[]{:S(2)}) copy-start(bf16[1,4,4,12,2048]{4,3,2,1,0:T(8,128)(2,1)} %get-tuple-element.51) | copy-start | bytes 2359300
  29.5 2.4 %copy-start.8 = (bf16[384,2048]{1,0:T(8,128)(2,1)S(1)}, bf16[384,2048]{1,0:T(8,128)(2,1)}, u32[]{:S(2)}) copy-start(bf16[384,2048]{1,0:T(8,128)(2,1)} %convert_element_type.158) | copy-start | bytes 4718596
  32.0 2.0 copy-start.11
  32.0 2.0 copy-start.12
  33.9 1.0 copy-start.9
  33.9 1.1 copy-start.10
  35.2 8.6 %copy-start.13 = (s32[48,3]{0,1:T(4,128)S(1)}, s32[48,3]{0,1:T(4,128)}, u32[]{:S(2)}) copy-start(s32[48,3]{0,1:T(4,128)} %param.11) | copy-start | bytes 1732
  35.2 8.6 %copy-start.14 = (s32[48]{0:T(128)S(1)}, s32[48]{0:T(128)}, u32[]{:S(2)}) copy-start(s32[48]{0:T(128)} %param.12) | copy-start | bytes 580
  36.4 13.8 %all-to-all-start = ((s32[16,1,128]{2,1,0:T(1,128)}), s32[16,1,128]{2,1,0:T(1,128)S(1)}, u32[]{:S(2)}, u32[]{:S(2)}) async-start(s32[16,1,128]{2,1,0:T(1,128)} %bitcast), calls=%async_computation | async-start | bytes 16384 | tf_op jit(solution)/shard_map/all_to_all | solution.py:139
  133.4 3.6 %copy-start.2 = (f32[4,2,256,144]{2,3,1,0:T(8,128)S(1)}, f32[4,2,256,144]{2,3,1,0:T(8,128)}, u32[]{:S(2)}) copy-start(f32[4,2,256,144]{2,3,1,0:T(8,128)} %all-reduce.2.cloned.1.call-done) | copy-start | bytes 3538948
  139.5 6.7 %slice-start = ((s8[6291456]{0:T(1024)(128)(4,1)}), s8[4194304]{0:T(1024)(128)(4,1)S(1)}, s32[]{:S(2)}) async-start(s8[6291456]{0:T(1024)(128)(4,1)} %bitcast.211), calls=%async_computation.3 | async-start | bytes 8388608
  141.7 4.6 %slice-start.1 = ((s8[6291456]{0:T(1024)(128)(4,1)}), s8[2097152]{0:T(1024)(128)(4,1)S(1)}, s32[]{:S(2)}) async-start(s8[6291456]{0:T(1024)(128)(4,1)} %bitcast.211), calls=%async_computation.4 | async-start | bytes 4194304
  196.4 2.8 %copy-start.1 = (f32[128,2,256]{2,1,0:T(2,128)S(1)}, f32[128,2,256]{2,1,0:T(2,128)}, u32[]{:S(2)}) copy-start(f32[128,2,256]{2,1,0:T(2,128)} %param.9) | copy-start | bytes 786436
Sparse Core Ops, SparseCore 0:
  36.5 96.7 all-reduce.1
where the time goes:
time: 206 us
  waiting for transfers between devices  88.8 us (43%)
  blocking collectives  33 us (16%)
  matrix products  29 us (14%)
  local copies, waits for them, and re-layouts  21.5 us (10%)
  between operations  14.6 us (7%)
  other arithmetic  11.7 us (6%)
  starting transfers between devices  7.44 us (4%)
    psum x1, waiting for transfers between devices, on_device(): blocks = lax.psum(partial_blocks, 'space')  83.1 us
    all_to_all x1, blocking collectives, on_device(): lax.all_to_all(picked, 'space', split_axis=1, concat_axis=1, tiled=True)  33 us
    dot_general x3, matrix products, project(): lax.dot_general(eig_colour[0], phased, site_dims, preferred_element_type=...  8.78 us
    gather x2, local copies, waits for them, and re-layouts, on_device(): picked = jnp.take(source, local_index, axis=1)  8.36 us
    all_to_all x1, starting transfers between devices, on_device(): lax.all_to_all(solver_order.reshape(devices, -1), 'space', split_axis=0,...  7.43 us
    dot_general x3, matrix products, project(): lax.dot_general(eig_colour[1], phased, site_dims, preferred_element_type=...  7.31 us
    all_to_all x1, waiting for transfers between devices, on_device(): lax.all_to_all(solver_order.reshape(devices, -1), 'space', split_axis=0,...  5.65 us
    convert_element_type x3, local copies, waits for them, and re-layouts, phased_rows(): return turned.astype(jnp.bfloat16).reshape(-1, turned.shape[-1])  4.12 us
  transfers between devices with their start and end apart: 2, of which 2 were waited for; matrix products, arithmetic and copies ran while one was open for 0% of the time, Pallas kernels for 0%

commit v1 on v0

--- a/solution.py
+++ b/solution.py
@@ -9,6 +9,18 @@
 EXTENT = 64
 MOMENTA = ((0, 0, 0), (1, 0, 0), (0, 1, 0), (0, 0, 1))
 PRECISE = lax.Precision.HIGHEST
+
+
+def in_blocks(x, dim, size):
+    dims = x.shape
+    parts = x.reshape(*dims[:dim], size, dims[dim] // size, *dims[dim + 1 :])
+    return jnp.moveaxis(parts, dim, 0)
+
+
+def joined_along(blocks, dim):
+    shape = list(blocks.shape[1:])
+    shape[dim] *= blocks.shape[0]
+    return jnp.moveaxis(blocks, 0, dim).reshape(shape)
 
 
 def phase_tables(offset, length):
@@ -136,9 +148,15 @@
         for colour in range(3)
     ]
     source = jnp.stack(colours, axis=1).astype(jnp.bfloat16).reshape(2 * 3 * 48, length)
-    wanted = lax.all_to_all(
-        solver_order.reshape(devices, -1), "space", split_axis=0, concat_axis=0, tiled=True
-    )
+    x = solver_order.reshape(devices, -1)
+    devices_2, index = (lax.axis_size("space"), lax.axis_index("space"))
+    pieces_2 = in_blocks(x, 0, devices_2)
+    gathered = [pieces_2[index]]
+    for step in range(1, devices_2):
+        sent = pieces_2[index ^ step]
+        gathered.append(lax.ppermute(sent, "space", [(i, i ^ step) for i in range(devices_2)]))
+    pieces_2 = jnp.stack(gathered)[index ^ jnp.arange(devices_2)]
+    wanted = joined_along(pieces_2, 0)
     local_index = wanted.reshape(length) - offset
     picked = jnp.take(source, local_index, axis=1)
     placed = lax.all_to_all(picked, "space", split_axis=1, concat_axis=1, tiled=True)

time: 206 us -> 207 us (level)
  waiting for transfers between devices: 88.8 us -> 73.1 us
  starting transfers between devices: 7.44 us -> 22.4 us
    ppermute x0 -> x15, starting transfers between devices: none -> 22.4 us  [on_device(): lax.ppermute(sent, 'space', [(i, i ^ step) for i in range(devices_2)])]
    psum x1, waiting for transfers between devices: 83.1 us -> 69.1 us  [on_device(): blocks = lax.psum(partial_blocks, 'space')]
    all_to_all x1 -> x0, starting transfers between devices: 7.43 us -> none  [on_device(): lax.all_to_all(solver_order.reshape(devices, -1), 'space', split_axis=0,...]
    all_to_all x1 -> x0, waiting for transfers between devices: 5.65 us -> none  [on_device(): lax.all_to_all(solver_order.reshape(devices, -1), 'space', split_axis=0,...]
    ppermute x0 -> x15, waiting for transfers between devices: none -> 3.96 us  [on_device(): lax.ppermute(sent, 'space', [(i, i ^ step) for i in range(devices_2)])]
  transfers between devices with their start and end apart: 2 -> 16, of which waited for: 2 -> 3; matrix products, arithmetic and copies ran while one was open for 0% -> 0% of each run, Pallas kernels for 0% -> 0%
where the time goes in v1:
time: 207 us; the launch traced here: 206 us
  waiting for transfers between devices  73.1 us (35%)
  blocking collectives  33 us (16%)
  matrix products  28.9 us (14%)
  starting transfers between devices  22.4 us (11%)
  local copies, waits for them, and re-layouts  22.2 us (11%)
  between operations  14.8 us (7%)
  other arithmetic  11.9 us (6%)
    psum x1, waiting for transfers between devices, on_device(): blocks = lax.psum(partial_blocks, 'space')  69.1 us
    all_to_all x1, blocking collectives, on_device(): lax.all_to_all(picked, 'space', split_axis=1, concat_axis=1, tiled=True)  33 us
    ppermute x15, starting transfers between devices, on_device(): lax.ppermute(sent, 'space', [(i, i ^ step) for i in range(devices_2)])  22.4 us
    dot_general x3, matrix products, project(): lax.dot_general(eig_colour[0], phased, site_dims, preferred_element_type=...  8.74 us
    gather x2, local copies, waits for them, and re-layouts, on_device(): picked = jnp.take(source, local_index, axis=1)  8.36 us
    dot_general x3, matrix products, project(): lax.dot_general(eig_colour[1], phased, site_dims, preferred_element_type=...  7.3 us
  transfers between devices with their start and end apart: 16, of which 3 were waited for; matrix products, arithmetic and copies ran while one was open for 0% of the time, Pallas kernels for 0%

profile of v1, /device:TPU:0, one launch (start us, length us, event | category | flops | bytes accessed | tf_op | source)
XLA Modules:
  0.0 206.3 jit_solution(3720682918315767384)
XLA Ops:
  6.8 1.5 bitcast_convert_fusion.5
  10.0 2.8 %add_convert_fusion.2 = (bf16[1,4,4,12,2048]{4,3,2,1,0:T(8,128)(2,1)S(1)}, bf16[1,4,4,12,2048]{4,3,2,1,0:T(8,128)(2,1)S(1)}, bf16[1,4,4,12,2048]{4,3,2,1,0:T(8,1...) fusion(f32[4,12,2048]{2,1,0:T(8,128)S(1)} %copy.83, ...), kind=kLoop, calls=%fused_computation.17 | loop fusion | flops 9437184 | bytes 7143424 | tf_op jit(solution)/shard_map/convert.13
  13.1 1.4 convert_element_type.148
  14.4 3.2 %fusion.33 = f32[384,256]{1,0:T(8,128)} fusion(bf16[384,2048]{1,0:T(8,128)(2,1)} %convert_element_type.148, bf16[2,3,256,2048]{3,2,1,0:T(8,128)(2,1)} %param.8), kind=kOutput, calls=%fused_computation.59 | convolution fusion | flops 402653184 | bytes 3014656 | tf_op jit(solution)/shard_map/dot_general | solution.py:54
  17.6 2.7 %fusion.29 = f32[384,256]{1,0:T(8,128)} fusion(bf16[384,2048]{1,0:T(8,128)(2,1)S(1)} %copy-done.6, bf16[2,3,256,2048]{3,2,1,0:T(8,128)(2,1)} %param.8), kind=kOutput, calls=%fused_computation.55 | convolution fusion | flops 402653184 | bytes 3014656 | tf_op jit(solution)/shard_map/dot_general | solution.py:57
  20.6 1.4 convert_element_type.153
  22.0 3.2 %fusion.25 = f32[384,256]{1,0:T(8,128)} fusion(bf16[384,2048]{1,0:T(8,128)(2,1)} %convert_element_type.153, bf16[2,3,256,2048]{3,2,1,0:T(8,128)(2,1)} %param.8), kind=kOutput, calls=%fused_computation.51 | convolution fusion | flops 402653184 | bytes 3014656 | tf_op jit(solution)/shard_map/dot_general | solution.py:54
  25.2 2.7 %fusion.21 = f32[384,256]{1,0:T(8,128)} fusion(bf16[384,2048]{1,0:T(8,128)(2,1)S(1)} %copy-done.7, bf16[2,3,256,2048]{3,2,1,0:T(8,128)(2,1)} %param.8), kind=kOutput, calls=%fused_computation.47 | convolution fusion | flops 402653184 | bytes 3014656 | tf_op jit(solution)/shard_map/dot_general | solution.py:57
  28.1 1.4 convert_element_type.158
  29.5 2.4 %fusion.17 = f32[384,256]{1,0:T(8,128)S(1)} fusion(bf16[384,2048]{1,0:T(8,128)(2,1)} %convert_element_type.158, bf16[2,3,256,2048]{3,2,1,0:T(8,128)(2,1)} %param.8), kind=kOutput, calls=%fused_computation.43 | convolution fusion | flops 402653184 | bytes 3014656 | tf_op jit(solution)/shard_map/dot_general | solution.py:54
  32.0 1.9 fusion.13
  34.0 0.8 copy-done.9
  35.2 1.1 pad_maximum_fusion.3
  36.6 3.1 %collective-permute-start.3 = (s32[1,128]{1,0:T(1,128)S(1)}, s32[1,128]{1,0:T(1,128)S(1)}, u32[]{:S(2)}, u32[]{:S(2)}) collective-permute-start(s32[1,128]{1,0:T(1,128)S(1)} %get-tuple-element.65), channel_id=1, source_target_pairs={{0,4},{1,5},{2,6},{3,7},{4,0},{5,1},{6,2},{7,3},{8,12},{9,13},{10,... | collective-permute-start | bytes 1544 | tf_op jit(solution)/shard_map/ppermute | solution.py:157
  39.7 2.1 %collective-permute-start.5 = (s32[1,128]{1,0:T(1,128)S(1)}, s32[1,128]{1,0:T(1,128)S(1)}, u32[]{:S(2)}, u32[]{:S(2)}) collective-permute-start(s32[1,128]{1,0:T(1,128)S(1)} %get-tuple-element.63), channel_id=1, source_target_pairs={{0,6},{1,7},{2,4},{3,5},{4,2},{5,3},{6,0},{7,1},{8,14},{9,15},{10,... | collective-permute-start | bytes 1544 | tf_op jit(solution)/shard_map/ppermute | solution.py:157
  42.4 2.7 %collective-permute-start.7 = (s32[1,128]{1,0:T(1,128)S(1)}, s32[1,128]{1,0:T(1,128)S(1)}, u32[]{:S(2)}, u32[]{:S(2)}) collective-permute-start(s32[1,128]{1,0:T(1,128)S(1)} %get-tuple-element.61), channel_id=1, source_target_pairs={{0,8},{1,9},{2,10},{3,11},{4,12},{5,13},{6,14},{7,15},{8,0},{9,1},... | collective-permute-start | bytes 1544 | tf_op jit(solution)/shard_map/ppermute | solution.py:157
  46.2 3.7 %collective-permute-start.9 = (s32[1,128]{1,0:T(1,128)S(1)}, s32[1,128]{1,0:T(1,128)S(1)}, u32[]{:S(2)}, u32[]{:S(2)}) collective-permute-start(s32[1,128]{1,0:T(1,128)S(1)} %get-tuple-element.59), channel_id=1, source_target_pairs={{0,10},{1,11},{2,8},{3,9},{4,14},{5,15},{6,12},{7,13},{8,2},{9,3},... | collective-permute-start | bytes 1544 | tf_op jit(solution)/shard_map/ppermute | solution.py:157
  49.9 3.3 %collective-permute-start.11 = (s32[1,128]{1,0:T(1,128)S(1)}, s32[1,128]{1,0:T(1,128)S(1)}, u32[]{:S(2)}, u32[]{:S(2)}) collective-permute-start(s32[1,128]{1,0:T(1,128)S(1)} %get-tuple-element.57), channel_id=1, source_target_pairs={{0,12},{1,13},{2,14},{3,15},{4,8},{5,9},{6,10},{7,11},{8,4},{9,5},... | collective-permute-start | bytes 1544 | tf_op jit(solution)/shard_map/ppermute | solution.py:157
  53.5 4.4 %collective-permute-start.13 = (s32[1,128]{1,0:T(1,128)S(1)}, s32[1,128]{1,0:T(1,128)S(1)}, u32[]{:S(2)}, u32[]{:S(2)}) collective-permute-start(s32[1,128]{1,0:T(1,128)S(1)} %get-tuple-element.55), channel_id=1, source_target_pairs={{0,14},{1,15},{2,12},{3,13},{4,10},{5,11},{6,8},{7,9},{8,6},{9,7},... | collective-permute-start | bytes 1544 | tf_op jit(solution)/shard_map/ppermute | solution.py:157
  58.0 1.2 collective-permute-start.1
  59.8 3.9 %collective-permute-done.14 = s32[1,128]{1,0:T(1,128)S(1)} collective-permute-done((s32[1,128]{1,0:T(1,128)S(1)}, s32[1,128]{1,0:T(1,128)S(1)}, u32[]{:S(2)}, u32[]{:S(2)}) %collective-permute-start.14) | collective-permute-done | bytes 544 | tf_op jit(solution)/shard_map/ppermute | solution.py:157
  63.7 0.6 gather_fusion
  64.3 69.1 %all-reduce.2.cloned.1.call-done = f32[4,2,256,144]{2,3,1,0:T(8,128)} async-done(((f32[4,2,256,144]{2,3,1,0:T(8,128)}), f32[4,2,256,144]{2,3,1,0:T(8,128)}) %all-reduce.2.cloned.1.call-update) | async-done | bytes 1179664 | tf_op jit(solution)/shard_map/psum | solution.py:142
  133.5 1.7 fusion.51
  135.2 1.7 fusion.53
  137.1 0.6 fusion.50
  137.7 0.6 fusion.52
  138.7 0.9 copy.91
  139.6 2.1 %convolution_bitcast_fusion = f32[4,2,256,48,12]{2,3,4,1,0:T(8,128)S(1)} fusion(f32[4,2,256,12,12]{2,1,4,3,0:T(2,128)S(1)} %bitcast.280, s32[48]{0:T(128)S(1)} %get-tuple-element.71), kind=kOutput, calls=%fused_computation.8 | convolution fusion | flops 169869888 | bytes 5898432 | tf_op jit(solution)/shard_map/mi,pqkij->pqkmj/dot_general | solution.py:95
  141.8 1.1 multiply_subtract_fusion
  142.9 2.5 %fusion.8 = bf16[4,2,256,12,12]{2,3,4,1,0:T(8,128)(2,1)S(1)} fusion(f32[4,1,256,48,12]{2,3,4,1,0:T(8,128)S(1)} %get-tuple-element.24, f32[4,1,256,48,12]{2,3,4,1,0:T(8,128)S(1)} %get-tuple-element.23, f32[48]{0:T(128)S(1)} %add_convert_fusion.4, s32[48]{0:T(128)S(1)} %get-tuple-element.70), kind=kOutput, calls=%fused_computation.32 | convolution fusion | flops 171345024 | bytes 5308800 | tf_op jit(solution)/shard_map/cm,pqkmj->pqkcj/dot_general | solution.py:102
  145.4 0.6 copy.95
  146.6 0.6 fusion.11
  147.2 0.6 fusion.15
  147.8 0.6 fusion.19
  148.4 0.6 fusion.23
  149.0 0.6 fusion.27
  149.6 0.6 fusion.31
  150.2 0.6 slice_add_fusion
  150.8 0.7 slice_add_fusion.1
  151.5 0.7 slice_subtract_fusion.2
  152.2 1.4 subtract_reduce_fusion.2
  153.9 0.8 copy.102
  154.8 7.5 %gather_fusion.1 = bf16[2048,288]{1,0:T(8,128)(2,1)S(1)} fusion(bf16[288,2048]{0,1:T(8,128)(2,1)S(1)} %copy.102, s32[2048]{0:T(1024)S(1)} %broadcast_clamp_fusion), kind=kCustom, calls=%fused_computation.1 | custom fusion | bytes 2367488 | tf_op jit(solution)/shard_map/jit(_take)/gather | solution.py:161
  162.2 0.9 copy.103
  163.3 33.0 %all_to_all.6 = bf16[288,16,128]{2,0,1:T(8,128)(2,1)S(1)} all-to-all(bf16[288,16,128]{2,0,1:T(8,128)(2,1)S(1)} %broadcast_select_fusion), channel_id=1, replica_groups=mesh['grp'=2,'space'=16] {'space'}, dimensions={1} | all-to-all | bytes 2359296 | tf_op jit(solution)/shard_map/all_to_all | solution.py:162
  196.7 0.8 reshape.965
  197.6 1.9 copy.105
  (106 shorter events, 7.3 us)
Async XLA Ops:
  6.5 126.9 %copy-start = (f32[128,2,256]{2,1,0:T(2,128)S(1)}, f32[128,2,256]{2,1,0:T(2,128)}, u32[]{:S(2)}) copy-start(f32[128,2,256]{2,1,0:T(2,128)} %param.9) | copy-start | bytes 786436
  6.5 126.9 %all-reduce.2.cloned.1.call-start = ((), (), s32[]{:S(2)}) async-start(), calls=%async_computation.1 | async-start | bytes 2359296 | tf_op jit(solution)/shard_map/psum | solution.py:142
  14.4 3.2 %copy-start.6 = (bf16[384,2048]{1,0:T(8,128)(2,1)S(1)}, bf16[384,2048]{1,0:T(8,128)(2,1)}, u32[]{:S(2)}) copy-start(bf16[384,2048]{1,0:T(8,128)(2,1)} %convert_element_type.148) | copy-start | bytes 4718596
  17.6 2.7 %copy-start.4 = (bf16[1,4,4,12,2048]{4,3,2,1,0:T(8,128)(2,1)S(1)}, bf16[1,4,4,12,2048]{4,3,2,1,0:T(8,128)(2,1)}, u32[]{:S(2)}) copy-start(bf16[1,4,4,12,2048]{4,3,2,1,0:T(8,128)(2,1)} %get-tuple-element.48) | copy-start | bytes 2359300
  17.6 2.7 %copy-start.5 = (bf16[1,4,4,12,2048]{4,3,2,1,0:T(8,128)(2,1)S(1)}, bf16[1,4,4,12,2048]{4,3,2,1,0:T(8,128)(2,1)}, u32[]{:S(2)}) copy-start(bf16[1,4,4,12,2048]{4,3,2,1,0:T(8,128)(2,1)} %get-tuple-element.49) | copy-start | bytes 2359300
  22.0 3.2 %copy-start.7 = (bf16[384,2048]{1,0:T(8,128)(2,1)S(1)}, bf16[384,2048]{1,0:T(8,128)(2,1)}, u32[]{:S(2)}) copy-start(bf16[384,2048]{1,0:T(8,128)(2,1)} %convert_element_type.153) | copy-start | bytes 4718596
  25.2 2.7 %copy-start.3 = (bf16[1,4,4,12,2048]{4,3,2,1,0:T(8,128)(2,1)S(1)}, bf16[1,4,4,12,2048]{4,3,2,1,0:T(8,128)(2,1)}, u32[]{:S(2)}) copy-start(bf16[1,4,4,12,2048]{4,3,2,1,0:T(8,128)(2,1)} %get-tuple-element.51) | copy-start | bytes 2359300
  29.5 2.4 %copy-start.8 = (bf16[384,2048]{1,0:T(8,128)(2,1)S(1)}, bf16[384,2048]{1,0:T(8,128)(2,1)}, u32[]{:S(2)}) copy-start(bf16[384,2048]{1,0:T(8,128)(2,1)} %convert_element_type.158) | copy-start | bytes 4718596
  31.9 2.0 copy-start.11
  32.0 2.0 copy-start.12
  33.9 1.0 copy-start.9
  33.9 1.1 copy-start.10
  35.2 1.3 copy-start.13
  35.2 9.9 %copy-start.14 = (s32[48,3]{0,1:T(4,128)S(1)}, s32[48,3]{0,1:T(4,128)}, u32[]{:S(2)}) copy-start(s32[48,3]{0,1:T(4,128)} %param.11) | copy-start | bytes 1732
  35.2 9.9 %copy-start.15 = (s32[48]{0:T(128)S(1)}, s32[48]{0:T(128)}, u32[]{:S(2)}) copy-start(s32[48]{0:T(128)} %param.12) | copy-start | bytes 580
  36.6 9.2 %collective-permute-start.3 = (s32[1,128]{1,0:T(1,128)S(1)}, s32[1,128]{1,0:T(1,128)S(1)}, u32[]{:S(2)}, u32[]{:S(2)}) collective-permute-start(s32[1,128]{1,0:T(1,128)S(1)} %get-tuple-element.65), channel_id=1, source_target_pairs={{0,4},{1,5},{2,6},{3,7},{4,0},{5,1},{6,2},{7,3},{8,12},{9,13},{10,... | collective-permute-start | bytes 1544 | tf_op jit(solution)/shard_map/ppermute | solution.py:157
  39.7 6.2 %collective-permute-start.4 = (s32[1,128]{1,0:T(1,128)S(1)}, s32[1,128]{1,0:T(1,128)S(1)}, u32[]{:S(2)}, u32[]{:S(2)}) collective-permute-start(s32[1,128]{1,0:T(1,128)S(1)} %get-tuple-element.64), channel_id=1, source_target_pairs={{0,5},{1,4},{2,7},{3,6},{4,1},{5,0},{6,3},{7,2},{8,13},{9,12},{10,... | collective-permute-start | bytes 1544 | tf_op jit(solution)/shard_map/ppermute | solution.py:157
  39.7 6.5 %collective-permute-start.5 = (s32[1,128]{1,0:T(1,128)S(1)}, s32[1,128]{1,0:T(1,128)S(1)}, u32[]{:S(2)}, u32[]{:S(2)}) collective-permute-start(s32[1,128]{1,0:T(1,128)S(1)} %get-tuple-element.63), channel_id=1, source_target_pairs={{0,6},{1,7},{2,4},{3,5},{4,2},{5,3},{6,0},{7,1},{8,14},{9,15},{10,... | collective-permute-start | bytes 1544 | tf_op jit(solution)/shard_map/ppermute | solution.py:157
  41.8 8.0 %collective-permute-start.6 = (s32[1,128]{1,0:T(1,128)S(1)}, s32[1,128]{1,0:T(1,128)S(1)}, u32[]{:S(2)}, u32[]{:S(2)}) collective-permute-start(s32[1,128]{1,0:T(1,128)S(1)} %get-tuple-element.62), channel_id=1, source_target_pairs={{0,7},{1,6},{2,5},{3,4},{4,3},{5,2},{6,1},{7,0},{8,15},{9,14},{10,... | collective-permute-start | bytes 1544 | tf_op jit(solution)/shard_map/ppermute | solution.py:157
  42.4 7.5 %collective-permute-start.7 = (s32[1,128]{1,0:T(1,128)S(1)}, s32[1,128]{1,0:T(1,128)S(1)}, u32[]{:S(2)}, u32[]{:S(2)}) collective-permute-start(s32[1,128]{1,0:T(1,128)S(1)} %get-tuple-element.61), channel_id=1, source_target_pairs={{0,8},{1,9},{2,10},{3,11},{4,12},{5,13},{6,14},{7,15},{8,0},{9,1},... | collective-permute-start | bytes 1544 | tf_op jit(solution)/shard_map/ppermute | solution.py:157
  45.8 7.3 %collective-permute-start.8 = (s32[1,128]{1,0:T(1,128)S(1)}, s32[1,128]{1,0:T(1,128)S(1)}, u32[]{:S(2)}, u32[]{:S(2)}) collective-permute-start(s32[1,128]{1,0:T(1,128)S(1)} %get-tuple-element.60), channel_id=1, source_target_pairs={{0,9},{1,8},{2,11},{3,10},{4,13},{5,12},{6,15},{7,14},{8,1},{9,0},... | collective-permute-start | bytes 1544 | tf_op jit(solution)/shard_map/ppermute | solution.py:157
  45.9 7.7 %collective-permute-start = (s32[1,128]{1,0:T(1,128)S(1)}, s32[1,128]{1,0:T(1,128)S(1)}, u32[]{:S(2)}, u32[]{:S(2)}) collective-permute-start(s32[1,128]{1,0:T(1,128)S(1)} %get-tuple-element.68), channel_id=1, source_target_pairs={{0,1},{1,0},{2,3},{3,2},{4,5},{5,4},{6,7},{7,6},{8,9},{9,8},{10,11... | collective-permute-start | bytes 1544 | tf_op jit(solution)/shard_map/ppermute | solution.py:157
  46.2 11.8 %collective-permute-start.9 = (s32[1,128]{1,0:T(1,128)S(1)}, s32[1,128]{1,0:T(1,128)S(1)}, u32[]{:S(2)}, u32[]{:S(2)}) collective-permute-start(s32[1,128]{1,0:T(1,128)S(1)} %get-tuple-element.59), channel_id=1, source_target_pairs={{0,10},{1,11},{2,8},{3,9},{4,14},{5,15},{6,12},{7,13},{8,2},{9,3},... | collective-permute-start | bytes 1544 | tf_op jit(solution)/shard_map/ppermute | solution.py:157
  49.9 8.1 %collective-permute-start.10 = (s32[1,128]{1,0:T(1,128)S(1)}, s32[1,128]{1,0:T(1,128)S(1)}, u32[]{:S(2)}, u32[]{:S(2)}) collective-permute-start(s32[1,128]{1,0:T(1,128)S(1)} %get-tuple-element.58), channel_id=1, source_target_pairs={{0,11},{1,10},{2,9},{3,8},{4,15},{5,14},{6,13},{7,12},{8,3},{9,2},... | collective-permute-start | bytes 1544 | tf_op jit(solution)/shard_map/ppermute | solution.py:157
  49.9 9.4 %collective-permute-start.11 = (s32[1,128]{1,0:T(1,128)S(1)}, s32[1,128]{1,0:T(1,128)S(1)}, u32[]{:S(2)}, u32[]{:S(2)}) collective-permute-start(s32[1,128]{1,0:T(1,128)S(1)} %get-tuple-element.57), channel_id=1, source_target_pairs={{0,12},{1,13},{2,14},{3,15},{4,8},{5,9},{6,10},{7,11},{8,4},{9,5},... | collective-permute-start | bytes 1544 | tf_op jit(solution)/shard_map/ppermute | solution.py:157
  53.1 6.6 %collective-permute-start.12 = (s32[1,128]{1,0:T(1,128)S(1)}, s32[1,128]{1,0:T(1,128)S(1)}, u32[]{:S(2)}, u32[]{:S(2)}) collective-permute-start(s32[1,128]{1,0:T(1,128)S(1)} %get-tuple-element.56), channel_id=1, source_target_pairs={{0,13},{1,12},{2,15},{3,14},{4,9},{5,8},{6,11},{7,10},{8,5},{9,4},... | collective-permute-start | bytes 1544 | tf_op jit(solution)/shard_map/ppermute | solution.py:157
  53.5 6.3 %collective-permute-start.13 = (s32[1,128]{1,0:T(1,128)S(1)}, s32[1,128]{1,0:T(1,128)S(1)}, u32[]{:S(2)}, u32[]{:S(2)}) collective-permute-start(s32[1,128]{1,0:T(1,128)S(1)} %get-tuple-element.55), channel_id=1, source_target_pairs={{0,14},{1,15},{2,12},{3,13},{4,10},{5,11},{6,8},{7,9},{8,6},{9,7},... | collective-permute-start | bytes 1544 | tf_op jit(solution)/shard_map/ppermute | solution.py:157
  58.0 5.7 %collective-permute-start.14 = (s32[1,128]{1,0:T(1,128)S(1)}, s32[1,128]{1,0:T(1,128)S(1)}, u32[]{:S(2)}, u32[]{:S(2)}) collective-permute-start(s32[1,128]{1,0:T(1,128)S(1)} %get-tuple-element.54), channel_id=1, source_target_pairs={{0,15},{1,14},{2,13},{3,12},{4,11},{5,10},{6,9},{7,8},{8,7},{9,6},... | collective-permute-start | bytes 1544 | tf_op jit(solution)/shard_map/ppermute | solution.py:157
  58.0 5.7 %collective-permute-start.1 = (s32[1,128]{1,0:T(1,128)S(1)}, s32[1,128]{1,0:T(1,128)S(1)}, u32[]{:S(2)}, u32[]{:S(2)}) collective-permute-start(s32[1,128]{1,0:T(1,128)S(1)} %get-tuple-element.67), channel_id=1, source_target_pairs={{0,2},{1,3},{2,0},{3,1},{4,6},{5,7},{6,4},{7,5},{8,10},{9,11},{10,... | collective-permute-start | bytes 1544 | tf_op jit(solution)/shard_map/ppermute | solution.py:157
  59.2 4.4 %collective-permute-start.2 = (s32[1,128]{1,0:T(1,128)S(1)}, s32[1,128]{1,0:T(1,128)S(1)}, u32[]{:S(2)}, u32[]{:S(2)}) collective-permute-start(s32[1,128]{1,0:T(1,128)S(1)} %get-tuple-element.66), channel_id=1, source_target_pairs={{0,3},{1,2},{2,1},{3,0},{4,7},{5,6},{6,5},{7,4},{8,11},{9,10},{10,... | collective-permute-start | bytes 1544 | tf_op jit(solution)/shard_map/ppermute | solution.py:157
  133.5 3.6 %copy-start.2 = (f32[4,2,256,144]{2,3,1,0:T(8,128)S(1)}, f32[4,2,256,144]{2,3,1,0:T(8,128)}, u32[]{:S(2)}) copy-start(f32[4,2,256,144]{2,3,1,0:T(8,128)} %all-reduce.2.cloned.1.call-done) | copy-start | bytes 3538948
  139.6 7.0 %slice-start = ((s8[6291456]{0:T(1024)(128)(4,1)}), s8[4194304]{0:T(1024)(128)(4,1)S(1)}, s32[]{:S(2)}) async-start(s8[6291456]{0:T(1024)(128)(4,1)} %bitcast.287), calls=%async_computation.2 | async-start | bytes 8388608
  141.8 4.8 %slice-start.1 = ((s8[6291456]{0:T(1024)(128)(4,1)}), s8[2097152]{0:T(1024)(128)(4,1)S(1)}, s32[]{:S(2)}) async-start(s8[6291456]{0:T(1024)(128)(4,1)} %bitcast.287), calls=%async_computation.3 | async-start | bytes 4194304
  196.7 2.8 %copy-start.1 = (f32[128,2,256]{2,1,0:T(2,128)S(1)}, f32[128,2,256]{2,1,0:T(2,128)}, u32[]{:S(2)}) copy-start(f32[128,2,256]{2,1,0:T(2,128)} %param.9) | copy-start | bytes 786436
Sparse Core Ops, SparseCore 0:
  36.5 96.9 all-reduce.1
